TPU v7x, 32 devices: a whole 2x2x4 slice. The times are simulated.
32 devices in a mesh: expert: 4 (over y, x), dp: 8 (over z, core).
Axes of the slice: x: 2, y: 2, z: 4, core: 2. Of those that a mesh axis runs over, the one named last changes fastest.
Arguments:
- acts: bfloat16 [32, 4, 16, 3584], P(('expert', 'dp')), may hold values from -6 to 6
- grad_out: bfloat16 [32, 4, 16, 1024], P(('expert', 'dp')), may hold values from -0.375 to 0.375
- routing_counts: int32 [32, 4], P(('expert', 'dp')), may hold values from 1 to 16, as said below
- left_basis: bfloat16 [4, 3584, 3584], P('expert', 'dp'), may hold values from -1 to 1, as said below
- right_basis: bfloat16 [4, 1024, 1024], P('expert'), may hold values from -1 to 1, as said below
- first_moment: float32 [4, 3584, 1024], P('expert', 'dp'), may hold values from -3 to 3
- second_moment: float32 [4, 3584, 1024], P('expert', 'dp'), may hold values from 0.05 to 2000
Outputs:
- step_delta: bfloat16 [4, 3584, 1024], P('expert', 'dp')
- first_out: float32 [4, 3584, 1024], P('expert', 'dp')
- second_out: float32 [4, 3584, 1024], P('expert', 'dp')
- expert_rms: float32 [4], P('expert')
Inputs may be any that keep to these rules, and one draw needn't show every extreme that they name: Slot s of shard i for expert e carries a routed token when s < routing_counts[i, e]; the other slots hold leftover values that belong to no token. In every shard some expert has all 16 slots live. `left_basis`: each expert's block is an orthogonal matrix rounded to bfloat16. `right_basis`: each expert's block is an orthogonal matrix rounded to bfloat16.
All inputs are finite; a program needn't handle non-finite values.
Results may differ from a plain program's by a relative error of at most 0.013.
Values may be sent and summed in bfloat16 or wider, within the bound.
A program may use at most 64 MiB of HBM per device.

v0:
```python
import jax
import jax.numpy as jnp
from jax import lax
from jax.sharding import PartitionSpec as P

BETA_ONE = 0.9
BETA_TWO = 0.95
EPS_DIVIDE = 1e-08
EPS_MEAN = 1e-06


def local(acts, grad_out, routing_counts, left_basis, right_basis, first_moment, second_moment):
    slot_count = acts.shape[2]
    slot_index = lax.broadcasted_iota(jnp.int32, routing_counts.shape + (slot_count,), 2)
    live_slots = (slot_index < routing_counts[:, :, None])[..., None]
    acts_live = jnp.where(live_slots, acts, jnp.zeros((), jnp.bfloat16))
    grads_live = jnp.where(live_slots, grad_out, jnp.zeros((), jnp.bfloat16))
    came_acts, came_grads = (
        lax.all_to_all(acts_live, "expert", split_axis=1, concat_axis=0, tiled=True),
        lax.all_to_all(grads_live, "expert", split_axis=1, concat_axis=0, tiled=True),
    )
    model_width = came_acts.shape[-1]
    hidden_width = came_grads.shape[-1]
    column_slabs = lax.all_to_all(came_acts, "dp", split_axis=3, concat_axis=0, tiled=True)
    grad_slabs = lax.all_gather(came_grads, "dp", axis=0, tiled=True)
    source_count = lax.axis_size("dp")
    column_slabs = column_slabs.reshape(source_count, -1, column_slabs.shape[-1])
    grad_slabs = grad_slabs.reshape(source_count, -1, hidden_width)
    partials = jnp.einsum(
        "stk,stf->skf", column_slabs, grad_slabs, preferred_element_type=jnp.float32
    )
    partials = lax.optimization_barrier(partials.astype(jnp.bfloat16))
    summed = jnp.sum(partials.astype(jnp.float32), axis=0)
    gradient = summed.astype(jnp.bfloat16)
    right_block = right_basis[0]
    left_rows = left_basis[0]
    right_turned = jnp.dot(gradient, right_block, preferred_element_type=jnp.float32).astype(
        jnp.bfloat16
    )
    basis_columns = left_rows
    rotated = lax.psum_scatter(
        jnp.einsum(
            "kc,kf->cf", basis_columns, right_turned, preferred_element_type=jnp.float32
        ).astype(jnp.bfloat16),
        "dp",
        scatter_dimension=0,
        tiled=True,
    ).astype(jnp.float32)
    first_new = BETA_ONE * first_moment[0] + (1.0 - BETA_ONE) * rotated
    second_new = BETA_TWO * second_moment[0] + (1.0 - BETA_TWO) * rotated * rotated
    direction = (first_new / (jnp.sqrt(second_new) + EPS_DIVIDE)).astype(jnp.bfloat16)
    restored = jnp.einsum(
        "kg,fg->kf", direction, right_block, preferred_element_type=jnp.float32
    ).astype(jnp.bfloat16)
    basis_columns = left_rows
    update = jnp.dot(
        basis_columns,
        lax.all_gather(restored, "dp", axis=0, tiled=True),
        preferred_element_type=jnp.float32,
    )
    squares = jnp.sum(update * update)
    cell_total = float(model_width * hidden_width)
    total_squares = lax.psum(squares, "dp")
    own_norm = jnp.sqrt(total_squares / cell_total + EPS_MEAN)
    norm_total = lax.psum(own_norm, "expert")
    mean_norm = norm_total / lax.axis_size("expert")
    step_delta = (-update / jnp.maximum(own_norm, mean_norm)).astype(jnp.bfloat16)
    return (step_delta[None], first_new[None], second_new[None], own_norm.reshape(1))


def solution(mesh):
    in_specs = (
        P(("expert", "dp"), None, None, None),
        P(("expert", "dp"), None, None, None),
        P(("expert", "dp"), None),
        P("expert", "dp", None),
        P("expert", None, None),
        P("expert", "dp", None),
        P("expert", "dp", None),
    )
    out_specs = (
        P("expert", "dp", None),
        P("expert", "dp", None),
        P("expert", "dp", None),
        P("expert"),
    )
    return jax.shard_map(local, mesh=mesh, in_specs=in_specs, out_specs=out_specs, check_vma=False)
```

profile of v0, /device:TPU:0, one launch (start us, length us, event | category | flops | bytes accessed | tf_op | source)
XLA Modules:
  0.0 312.0 jit_solution(15991708466216752481)
XLA Ops:
  9.1 10.1 %all_to_all.39 = bf16[1,4,16,1024]{3,2,0,1:T(8,128)(2,1)} all-to-all(bf16[1,4,16,1024]{3,2,0,1:T(8,128)(2,1)S(1)} %bitcast_select_fusion.1), channel_id=1, replica_groups=mesh['expert'=4,'dp'=8] {'expert'}, dimensions={1} | all-to-all | bytes 262144 | tf_op jit(solution)/shard_map/all_to_all | solution.py:20
  20.5 10.0 %all_to_all.40 = bf16[1,4,16,3584]{3,2,0,1:T(8,128)(2,1)} all-to-all(bf16[1,4,16,3584]{3,2,0,1:T(8,128)(2,1)S(1)} %bitcast_select_fusion), channel_id=1, replica_groups=mesh['expert'=4,'dp'=8] {'expert'}, dimensions={1} | all-to-all | bytes 917504 | tf_op jit(solution)/shard_map/all_to_all | solution.py:19
  30.5 5.3 %copy.31 = bf16[4,1,16,3584]{2,0,1,3:T(4,128)(2,1)} copy(bf16[4,1,16,3584]{3,2,0,1:T(8,128)(2,1)} %bitcast.64) | data formatting | bytes 917504 | tf_op jit(solution)/shard_map/all_to_all | solution.py:19
  35.8 6.0 %reshape.63 = bf16[8,2,14336]{2,1,0:T(2,128)(2,1)} reshape(bf16[3584,1,4,16]{3,2,1,0:T(4,128)(2,1)} %bitcast.60) | data formatting | bytes 917504
  41.7 18.9 %all_to_all.41 = bf16[8,2,14336]{2,1,0:T(2,128)(2,1)} all-to-all(bf16[8,2,14336]{2,1,0:T(2,128)(2,1)} %reshape.63), channel_id=1, replica_groups=mesh['expert'=4,'dp'=8] {'dp'}, dimensions={0} | all-to-all | bytes 917504 | tf_op jit(solution)/shard_map/all_to_all | solution.py:24
  60.7 5.1 %reshape.64 = bf16[3584,1,4,16]{3,2,1,0:T(4,128)(2,1)} reshape(bf16[8,2,14336]{2,1,0:T(2,128)(2,1)} %all_to_all.41) | data formatting | bytes 917504
  65.7 5.1 %copy.38 = bf16[4,1,16,8,448]{4,3,2,0,1:T(8,128)(2,1)} copy(bf16[4,1,16,8,448]{2,0,4,3,1:T(4,128)(2,1)} %bitcast.61) | data formatting | bytes 917504 | tf_op jit(solution)/shard_map/all_to_all | solution.py:24
  72.8 6.5 %convolution_convert_fusion.1 = bf16[8,448,1024]{2,1,0:T(8,128)(2,1)} fusion(bf16[8,64,448]{2,1,0:T(8,128)(2,1)} %bitcast.62, bf16[8,64,1024]{2,1,0:T(8,128)(2,1)} %bitcast.65), kind=kOutput, calls=%fused_computation.2 | convolution fusion | flops 473432064 | bytes 8847360 | tf_op jit(solution)/shard_map/stk,stf->skf/dot_general | solution.py:29
  79.3 6.0 %reduce_sum.21 = bf16[448,1024]{1,0:T(8,128)(2,1)} reduce(bf16[8,448,1024]{2,1,0:T(8,128)(2,1)} %convolution_convert_fusion.1, bf16[]{:T(256)} %constant.4.clone.1), dimensions={0}, to_apply=%region_0.1 | reduce | flops 3211264 | bytes 8257538 | tf_op jit(solution)/shard_map/reduce_sum | solution.py:33
  85.3 9.9 %fusion = bf16[3584,1024]{0,1:T(8,128)(2,1)} fusion(bf16[1,448,3584]{2,1,0:T(8,128)(2,1)S(1)} %copy-done, bf16[448,1024]{1,0:T(8,128)(2,1)} %reduce_sum.21, bf16[1,1024,1024]{2,1,0:T(8,128)(2,1)} %param.11), kind=kOutput, calls=%fused_computation.1 | convolution fusion | flops 4231987200 | bytes 13565952 | tf_op jit(solution)/shard_map/kc,kf->cf/dot_general | solution.py:42
  95.2 10.4 %copy.39 = bf16[3584,1024]{1,0:T(8,128)(2,1)} copy(bf16[3584,1024]{0,1:T(8,128)(2,1)} %fusion) | data formatting | bytes 14680064
  105.9 2.9 copy.29
  108.8 3.0 copy.35
  111.8 70.9 %reduce-scatter.4.cloned.1.call-done = bf16[448,1024]{1,0:T(8,128)(2,1)} async-done(((bf16[3584,1024]{1,0:T(8,128)(2,1)}), bf16[448,1024]{1,0:T(8,128)(2,1)}) %reduce-scatter.4.cloned.1.call-update) | async-done | bytes 917520
  182.6 2.2 copy.40
  184.9 6.4 %fusion.13 = bf16[448,1024]{1,0:T(8,128)(2,1)} fusion(bf16[1,1024,1024]{2,1,0:T(8,128)(2,1)} %param.11, bf16[448,1024]{0,1:T(8,128)(2,1)} %copy.40, f32[1,448,1024]{1,2,0:T(8,128)} %copy.29, f32[1,448,1024]{1,2,0:T(8,128)} %copy.35), kind=kOutput, calls=%fused_computation.18 | convolution fusion | flops 945029120 | bytes 7602176 | tf_op jit(solution)/shard_map/kg,fg->kf/dot_general | solution.py:52
  191.3 5.4 %fusion.17 = (f32[1,448,1024]{1,2,0:T(8,128)}, f32[1,448,1024]{1,2,0:T(8,128)}) fusion(bf16[448,1024]{0,1:T(8,128)(2,1)} %copy.40, f32[1,448,1024]{1,2,0:T(8,128)} %copy.35, f32[1,448,1024]{1,2,0:T(8,128)} %copy.29), kind=kLoop, calls=%fused_computation.20 | loop fusion | flops 3670016 | bytes 8257536 | tf_op jit(solution)/shard_map/broadcast_in_dim | solution.py:68
  196.7 3.0 copy.36
  199.7 63.6 %all-gather.4.cloned.1.call-done = bf16[3584,1024]{1,0:T(8,128)(2,1)} async-done(((bf16[448,1024]{1,0:T(8,128)(2,1)}), bf16[3584,1024]{1,0:T(8,128)(2,1)}) %all-gather.4.cloned.1.call-update) | async-done | bytes 7340048 | tf_op jit(solution)/shard_map/all_gather | solution.py:58
  263.3 8.4 %multiply_reduce_fusion = (f32[]{:T(128)}, f32[1024,448]{0,1:T(8,128)}) fusion(bf16[3584,1024]{1,0:T(8,128)(2,1)} %all-gather.4.cloned.1.call-done, bf16[1,448,3584]{2,1,0:T(8,128)(2,1)S(1)} %copy-done), kind=kOutput, calls=%fused_computation.16 | convolution fusion | flops 3289251840 | bytes 12386308 | tf_op jit(solution)/shard_map/dot_general | solution.py:56
  271.6 14.7 %psum.14 = f32[]{:T(128)} all-reduce(f32[]{:T(128)} %get-tuple-element.22), channel_id=1, replica_groups=mesh['expert'=4,'dp'=8] {'dp'}, use_global_device_ids=true, to_apply=%region_3.4 | all-reduce | flops 1 | bytes 8 | tf_op jit(solution)/shard_map/psum | solution.py:63
  287.0 2.8 copy.37
  289.8 11.2 %psum.15 = f32[]{:T(128)} all-reduce(f32[]{:T(128)} %sqrt.7), channel_id=1, replica_groups=mesh['expert'=4,'dp'=8] {'expert'}, use_global_device_ids=true, to_apply=%region_4.5 | all-reduce | flops 1 | bytes 8 | tf_op jit(solution)/shard_map/psum | solution.py:65
  301.7 2.6 fusion.18
  (13 shorter events, 5.4 us)
Async XLA Ops:
  7.2 78.1 %copy-start = (bf16[1,448,3584]{2,1,0:T(8,128)(2,1)S(1)}, bf16[1,448,3584]{2,1,0:T(8,128)(2,1)}, u32[]{:S(2)}) copy-start(bf16[1,448,3584]{2,1,0:T(8,128)(2,1)} %param.10) | copy-start | bytes 9633796
  7.2 65.7 %all-gather.6.cloned.1.call-start = ((), (), s32[]{:S(2)}) async-start(), calls=%async_computation.5 | async-start | bytes 1179648 | tf_op jit(solution)/shard_map/all_gather | solution.py:25
  19.3 163.3 %reduce-scatter.4.cloned.1.call-start = ((), (), s32[]{:S(2)}) async-start(), calls=%async_computation.6 | async-start | bytes 8257536
  105.6 157.7 %all-gather.4.cloned.1.call-start = ((), (), s32[]{:S(2)}) async-start(), calls=%async_computation.4 | async-start | bytes 8257536 | tf_op jit(solution)/shard_map/all_gather | solution.py:58
Sparse Core Ops, SparseCore 0:
  19.4 21.7 all-gather.5
  105.7 76.8 reduce-scatter.3
  191.4 71.7 all-gather.3
where the time goes:
time: 313 us; the launch traced here: 312 us
  waiting for transfers between devices  134 us (43%)
  blocking collectives  65 us (21%)
  local copies, waits for them, and re-layouts  47.8 us (15%)
  matrix products  31.1 us (10%)
  other arithmetic  17.1 us (5%)
  between operations  16.3 us (5%)
    unnamed x4, waiting for transfers between devices  70.9 us
    all_gather x1, waiting for transfers between devices, local(): lax.all_gather(restored, 'dp', axis=0, tiled=True)  63.6 us
    unnamed x10, local copies, waits for them, and re-layouts  35.4 us
    all_to_all x1, blocking collectives, local(): lax.all_to_all(came_acts, 'dp', split_axis=3, concat_axis=0, tiled=True)  18.9 us
    psum x1, blocking collectives, local(): total_squares = lax.psum(squares, 'dp')  14.7 us
    psum x1, blocking collectives, local(): norm_total = lax.psum(own_norm, 'expert')  11.2 us
    all_to_all x1, blocking collectives, local(): lax.all_to_all(grads_live, 'expert', split_axis=1, concat_axis=0, tiled=T...  10.1 us
    all_to_all x1, blocking collectives, local(): lax.all_to_all(acts_live, 'expert', split_axis=1, concat_axis=0, tiled=True)  10 us
  transfers between devices with their start and end apart: 3, of which 2 were waited for; matrix products, arithmetic and copies ran while one was open for 12% of the time, Pallas kernels for 0%

commit v1 on v0

--- a/solution.py
+++ b/solution.py
@@ -21,7 +21,10 @@
     )
     model_width = came_acts.shape[-1]
     hidden_width = came_grads.shape[-1]
-    column_slabs = lax.all_to_all(came_acts, "dp", split_axis=3, concat_axis=0, tiled=True)
+    size = lax.axis_size("dp")
+    blocks = jnp.stack(jnp.split(came_acts, size, axis=3), axis=0)
+    blocks = lax.all_to_all(blocks, "dp", split_axis=0, concat_axis=0)
+    column_slabs = jnp.concatenate(blocks, axis=0)
     grad_slabs = lax.all_gather(came_grads, "dp", axis=0, tiled=True)
     source_count = lax.axis_size("dp")
     column_slabs = column_slabs.reshape(source_count, -1, column_slabs.shape[-1])

time: 313 us -> 303 us (0.968)
  blocking collectives: 65 us -> 48.6 us
  local copies, waits for them, and re-layouts: 47.8 us -> 31.5 us
  waiting for transfers between devices: 134 us -> 146 us
  starting transfers between devices: 0.3 us -> 9.61 us
    all_to_all x3 -> x1, blocking collectives: 39.1 us -> 22.7 us  [local(): blocks = lax.all_to_all(blocks, 'dp', split_axis=0, concat_axis=0)]
    all_to_all x3 -> x0, local copies, waits for them, and re-layouts: 12.4 us -> none  [the longest x2 7.1 us: local(): lax.all_to_all(came_acts, 'dp', split_axis=3, concat_axis=0, tiled=True)]
    all_to_all x0 -> x2, starting transfers between devices: none -> 9.31 us  [the longest x1 5.19 us: local(): lax.all_to_all(grads_live, 'expert', split_axis=1, concat_axis=0, tiled=T...]
    all_to_all x0 -> x2, waiting for transfers between devices: none -> 8.64 us  [the longest x1 5.5 us: local(): lax.all_to_all(acts_live, 'expert', split_axis=1, concat_axis=0, tiled=True)]
    unnamed x10 -> x17, local copies, waits for them, and re-layouts: 35.4 us -> 30.5 us
  transfers between devices with their start and end apart: 3 -> 5, of which waited for: 2 -> 4; matrix products, arithmetic and copies ran while one was open for 12% -> 8% of each run, Pallas kernels for 0% -> 0%
where the time goes in v1:
time: 303 us; the launch traced here: 302 us
  waiting for transfers between devices  146 us (48%)
  blocking collectives  48.6 us (16%)
  local copies, waits for them, and re-layouts  31.5 us (10%)
  matrix products  31.1 us (10%)
  other arithmetic  18.5 us (6%)
  between operations  16.3 us (5%)
  starting transfers between devices  9.61 us (3%)
    unnamed x4, waiting for transfers between devices  73.7 us
    all_gather x1, waiting for transfers between devices, local(): lax.all_gather(restored, 'dp', axis=0, tiled=True)  63.6 us
    unnamed x17, local copies, waits for them, and re-layouts  30.5 us
    all_to_all x1, blocking collectives, local(): blocks = lax.all_to_all(blocks, 'dp', split_axis=0, concat_axis=0)  22.7 us
    psum x1, blocking collectives, local(): total_squares = lax.psum(squares, 'dp')  14.7 us
    psum x1, blocking collectives, local(): norm_total = lax.psum(own_norm, 'expert')  11.2 us
    dot_general x1, matrix products, local(): jnp.einsum('kc,kf->cf', basis_columns, right_turned, preferred_element_ty...  9.91 us
    dot_general x1, matrix products, local(): jnp.dot(basis_columns, lax.all_gather(restored, 'dp', axis=0, tiled=True)...  8.39 us
  transfers between devices with their start and end apart: 5, of which 4 were waited for; matrix products, arithmetic and copies ran while one was open for 8% of the time, Pallas kernels for 0%

profile of v1, /device:TPU:0, one launch (start us, length us, event | category | flops | bytes accessed | tf_op | source)
XLA Modules:
  0.0 301.6 jit_solution(18418282786657525008)
XLA Ops:
  8.1 1.7 bitcast_select_fusion.1
  9.8 5.2 %all-to-all-start.2 = ((bf16[1,4,16,1024]{3,2,0,1:T(8,128)(2,1)}), bf16[1,4,16,1024]{3,2,0,1:T(8,128)(2,1)S(1)}, u32[]{:S(2)}, u32[]{:S(2)}) async-start(bf16[1,4,16,1024]{3,2,0,1:T(8,128)(2,1)} %bitcast_select_fusion.1), calls=%async_computation.2 | async-start | bytes 262144 | tf_op jit(solution)/shard_map/all_to_all | solution.py:20
  15.0 1.9 bitcast_select_fusion
  16.9 3.1 %all-to-all-done.2 = bf16[1,4,16,1024]{3,2,0,1:T(8,128)(2,1)S(1)} async-done(((bf16[1,4,16,1024]{3,2,0,1:T(8,128)(2,1)}), bf16[1,4,16,1024]{3,2,0,1:T(8,128)(2,1)S(1)}, u32[]{:S(2)}, u32[]{:S(2)}) %all-to-all-start.2) | async-done | bytes 131104 | tf_op jit(solution)/shard_map/all_to_all | solution.py:20
  20.0 4.1 %all-to-all-start = ((bf16[1,4,16,3584]{3,2,0,1:T(8,128)(2,1)}), bf16[1,4,16,3584]{3,2,0,1:T(8,128)(2,1)}, u32[]{:S(2)}, u32[]{:S(2)}) async-start(bf16[1,4,16,3584]{3,2,0,1:T(8,128)(2,1)} %bitcast_select_fusion), calls=%async_computation | async-start | bytes 917504 | tf_op jit(solution)/shard_map/all_to_all | solution.py:19
  24.9 5.5 %all-to-all-done = bf16[1,4,16,3584]{3,2,0,1:T(8,128)(2,1)} async-done(((bf16[1,4,16,3584]{3,2,0,1:T(8,128)(2,1)}), bf16[1,4,16,3584]{3,2,0,1:T(8,128)(2,1)}, u32[]{:S(2)}, u32[]{:S(2)}) %all-to-all-start) | async-done | bytes 458784 | tf_op jit(solution)/shard_map/all_to_all | solution.py:19
  37.7 22.7 %all_to_all.29 = bf16[8,4,1,16,448]{4,3,1,2,0:T(8,128)(2,1)} all-to-all(bf16[8,4,1,16,448]{4,3,1,2,0:T(8,128)(2,1)S(1)} %fusion.21), channel_id=1, replica_groups=mesh['expert'=4,'dp'=8] {'dp'}, dimensions={0} | all-to-all | bytes 917504 | tf_op jit(solution)/shard_map/all_to_all | solution.py:26
  60.4 6.4 %convolution_convert_fusion.1 = bf16[8,448,1024]{2,1,0:T(8,128)(2,1)} fusion(bf16[8,64,448]{2,1,0:T(8,128)(2,1)} %bitcast.88, bf16[8,64,1024]{2,1,0:T(8,128)(2,1)} %bitcast.89), kind=kOutput, calls=%fused_computation.2 | convolution fusion | flops 473432064 | bytes 8847360 | tf_op jit(solution)/shard_map/stk,stf->skf/dot_general | solution.py:32
  66.9 6.0 %reduce_sum.21 = bf16[448,1024]{1,0:T(8,128)(2,1)} reduce(bf16[8,448,1024]{2,1,0:T(8,128)(2,1)} %convolution_convert_fusion.1, bf16[]{:T(256)} %constant.4.clone.1), dimensions={0}, to_apply=%region_0.1 | reduce | flops 3211264 | bytes 8257538 | tf_op jit(solution)/shard_map/reduce_sum | solution.py:36
  72.9 9.9 %fusion = bf16[3584,1024]{0,1:T(8,128)(2,1)} fusion(bf16[1,448,3584]{2,1,0:T(8,128)(2,1)S(1)} %copy-done, bf16[448,1024]{1,0:T(8,128)(2,1)} %reduce_sum.21, bf16[1,1024,1024]{2,1,0:T(8,128)(2,1)} %param.11), kind=kOutput, calls=%fused_computation.1 | convolution fusion | flops 4231987200 | bytes 13565952 | tf_op jit(solution)/shard_map/kc,kf->cf/dot_general | solution.py:45
  82.8 10.4 %copy.21 = bf16[3584,1024]{1,0:T(8,128)(2,1)} copy(bf16[3584,1024]{0,1:T(8,128)(2,1)} %fusion) | data formatting | bytes 14680064
  93.4 2.9 copy.15
  96.4 2.8 copy.18
  99.2 73.0 %reduce-scatter.4.cloned.1.call-done = bf16[448,1024]{1,0:T(8,128)(2,1)} async-done(((bf16[3584,1024]{1,0:T(8,128)(2,1)}), bf16[448,1024]{1,0:T(8,128)(2,1)}) %reduce-scatter.4.cloned.1.call-update) | async-done | bytes 917520
  172.2 2.2 copy.22
  174.4 6.4 %fusion.13 = bf16[448,1024]{1,0:T(8,128)(2,1)} fusion(bf16[1,1024,1024]{2,1,0:T(8,128)(2,1)} %param.11, bf16[448,1024]{0,1:T(8,128)(2,1)} %copy.22, f32[1,448,1024]{1,2,0:T(8,128)} %copy.15, f32[1,448,1024]{1,2,0:T(8,128)} %copy.18), kind=kOutput, calls=%fused_computation.18 | convolution fusion | flops 945029120 | bytes 7602176 | tf_op jit(solution)/shard_map/kg,fg->kf/dot_general | solution.py:55
  180.9 5.4 %fusion.17 = (f32[1,448,1024]{1,2,0:T(8,128)}, f32[1,448,1024]{1,2,0:T(8,128)}) fusion(bf16[448,1024]{0,1:T(8,128)(2,1)} %copy.22, f32[1,448,1024]{1,2,0:T(8,128)} %copy.18, f32[1,448,1024]{1,2,0:T(8,128)} %copy.15), kind=kLoop, calls=%fused_computation.20 | loop fusion | flops 3670016 | bytes 8257536 | tf_op jit(solution)/shard_map/broadcast_in_dim | solution.py:71
  186.3 3.0 copy.19
  189.3 63.6 %all-gather.4.cloned.1.call-done = bf16[3584,1024]{1,0:T(8,128)(2,1)} async-done(((bf16[448,1024]{1,0:T(8,128)(2,1)}), bf16[3584,1024]{1,0:T(8,128)(2,1)}) %all-gather.4.cloned.1.call-update) | async-done | bytes 7340048 | tf_op jit(solution)/shard_map/all_gather | solution.py:61
  252.8 8.4 %multiply_reduce_fusion = (f32[]{:T(128)}, f32[1024,448]{0,1:T(8,128)}) fusion(bf16[3584,1024]{1,0:T(8,128)(2,1)} %all-gather.4.cloned.1.call-done, bf16[1,448,3584]{2,1,0:T(8,128)(2,1)S(1)} %copy-done), kind=kOutput, calls=%fused_computation.16 | convolution fusion | flops 3289251840 | bytes 12386308 | tf_op jit(solution)/shard_map/dot_general | solution.py:59
  261.2 14.7 %psum.14 = f32[]{:T(128)} all-reduce(f32[]{:T(128)} %get-tuple-element.14), channel_id=1, replica_groups=mesh['expert'=4,'dp'=8] {'dp'}, use_global_device_ids=true, to_apply=%region_3.4 | all-reduce | flops 1 | bytes 8 | tf_op jit(solution)/shard_map/psum | solution.py:66
  276.6 2.8 copy.20
  279.4 11.2 %psum.15 = f32[]{:T(128)} all-reduce(f32[]{:T(128)} %sqrt.7), channel_id=1, replica_groups=mesh['expert'=4,'dp'=8] {'expert'}, use_global_device_ids=true, to_apply=%region_4.5 | all-reduce | flops 1 | bytes 8 | tf_op jit(solution)/shard_map/psum | solution.py:68
  291.3 2.6 fusion.18
  (20 shorter events, 9.1 us)
Async XLA Ops:
  7.2 65.7 %copy-start = (bf16[1,448,3584]{2,1,0:T(8,128)(2,1)S(1)}, bf16[1,448,3584]{2,1,0:T(8,128)(2,1)}, u32[]{:S(2)}) copy-start(bf16[1,448,3584]{2,1,0:T(8,128)(2,1)} %param.10) | copy-start | bytes 9633796
  9.8 10.2 %all-to-all-start.2 = ((bf16[1,4,16,1024]{3,2,0,1:T(8,128)(2,1)}), bf16[1,4,16,1024]{3,2,0,1:T(8,128)(2,1)S(1)}, u32[]{:S(2)}, u32[]{:S(2)}) async-start(bf16[1,4,16,1024]{3,2,0,1:T(8,128)(2,1)} %bitcast_select_fusion.1), calls=%async_computation.2 | async-start | bytes 262144 | tf_op jit(solution)/shard_map/all_to_all | solution.py:20
  20.0 4.2 %copy-start.1 = (bf16[1,4,16,1024]{3,2,0,1:T(8,128)(2,1)}, bf16[1,4,16,1024]{3,2,0,1:T(8,128)(2,1)S(1)}, u32[]{:S(2)}) copy-start(bf16[1,4,16,1024]{3,2,0,1:T(8,128)(2,1)S(1)} %all-to-all-done.2) | copy-start | bytes 393220
  20.0 10.4 %all-to-all-start = ((bf16[1,4,16,3584]{3,2,0,1:T(8,128)(2,1)}), bf16[1,4,16,3584]{3,2,0,1:T(8,128)(2,1)}, u32[]{:S(2)}, u32[]{:S(2)}) async-start(bf16[1,4,16,3584]{3,2,0,1:T(8,128)(2,1)} %bitcast_select_fusion), calls=%async_computation | async-start | bytes 917504 | tf_op jit(solution)/shard_map/all_to_all | solution.py:19
  24.1 36.3 %all-gather.6.cloned.1.call-start = ((), (), s32[]{:S(2)}) async-start(), calls=%async_computation.5 | async-start | bytes 1179648 | tf_op jit(solution)/shard_map/all_gather | solution.py:28
  24.9 147.3 %reduce-scatter.4.cloned.1.call-start = ((), (), s32[]{:S(2)}) async-start(), calls=%async_computation.6 | async-start | bytes 8257536
  93.2 159.7 %all-gather.4.cloned.1.call-start = ((), (), s32[]{:S(2)}) async-start(), calls=%async_computation.4 | async-start | bytes 8257536 | tf_op jit(solution)/shard_map/all_gather | solution.py:61
Sparse Core Ops, SparseCore 0:
  27.1 28.3 all-gather.5
  93.3 78.8 reduce-scatter.3
  181.0 71.8 all-gather.3
